TPU v7x, 32 devices: a whole 2x2x4 slice. The times are simulated.
32 devices in a mesh: gx: 4 (over z), yz: 8 (over y, x, core).
Axes of the slice: x: 2, y: 2, z: 4, core: 2. Of those that a mesh axis runs over, the one named last changes fastest.
Arguments:
- brick_ids: int32 [4096, 1], P(('gx', 'yz')), may hold values from 0 to 31; in each aligned block of 128 rows (0 to 127, 128 to 255, ...) at most 4 rows name the same one
- voxel_offset: int32 [4096, 256], P(('gx', 'yz')), may hold values from 0 to 4095
- fractions: float32 [4096, 3, 256], P(('gx', 'yz')), may hold values from 0 to 1
- normals: float32 [4096, 3, 256], P(('gx', 'yz')), may hold values from -6 to 6
- point_weight: float32 [4096, 256], P(('gx', 'yz')), may hold values from 0.1 to 10
- tile_count: int32 [32], P(('gx', 'yz')), may hold values from 96 to 128, as said below
Outputs:
- rhs: float32 [16, 64, 128], P('gx', 'yz')
- screen: float32 [16, 64, 128], P('gx', 'yz')
Inputs may be any that keep to these rules, and one draw needn't show every extreme that they name: `brick_ids`: brick b belongs to index b // 8 of gx and b % 8 of yz. Among the 128 tile slots of one device no brick is named more than 4 times. `tile_count`: some device has all its slots valid in every draw.
All inputs are finite; a program needn't handle non-finite values.
Results may differ from a plain program's by a relative error of at most 0.0039.
Values sent between devices are 32-bit elements; how exact they have to be, the bound alone decides.
A program may use at most 64 MiB of HBM per device.

v0:
```python
import jax
import jax.numpy as jnp
from jax import lax
from jax.sharding import PartitionSpec as P

BX = 4
BY = 8
BZ = 128


def passed_along(value, axis, steps):
    count = lax.axis_size(axis)
    first, last = (max(0, -steps), min(count, count - steps))
    return lax.ppermute(value, axis, [(source, source + steps) for source in range(first, last)])


def spline(frac):
    weights = [0.5 * (1.0 - frac) ** 2, 0.75 - (frac - 0.5) ** 2, 0.5 * frac * frac]
    slopes = [frac - 1.0, 1.0 - 2.0 * frac, frac]
    return (weights, slopes)


def splat_block(carry, points):
    rhs_acc, screen_acc = carry
    channels = jnp.transpose(points, (1, 0, 2)).reshape(8, -1)
    offset = channels[0].astype(jnp.int32)
    cell_x = offset // (BY * BZ)
    cell_y = offset // BZ % BY
    cell_z = offset % BZ
    wx, gx = spline(channels[1])
    wy, gy = spline(channels[2])
    wz, gz = spline(channels[3])
    nx = channels[4]
    ny = channels[5]
    nz = channels[6]
    weight = channels[7]
    plane_rows = jnp.arange((BX + 2) * (BY + 2), dtype=jnp.int32)[:, None]
    depth_cols = jnp.arange(BZ, dtype=jnp.int32)[None, :]
    count = offset.shape[0]
    a_twelve = jnp.zeros(((BX + 2) * (BY + 2), count), jnp.float32)
    a_three = jnp.zeros_like(a_twelve)
    a_screen = jnp.zeros_like(a_twelve)
    for first in range(3):
        for second in range(3):
            target = ((cell_x + first) * (BY + 2) + cell_y + second)[None, :]
            hit = plane_rows == target
            term_twelve = nx * gx[first] * wy[second] + ny * wx[first] * gy[second]
            term_three = nz * wx[first] * wy[second]
            term_screen = weight * wx[first] * wy[second]
            a_twelve = a_twelve + jnp.where(hit, term_twelve[None, :], 0.0)
            a_three = a_three + jnp.where(hit, term_three[None, :], 0.0)
            a_screen = a_screen + jnp.where(hit, term_screen[None, :], 0.0)
    z_value = jnp.zeros((count, BZ), jnp.float32)
    z_slope = jnp.zeros_like(z_value)
    for third in range(3):
        hit = (cell_z + third - 1)[:, None] == depth_cols
        z_value = z_value + jnp.where(hit, wz[third][:, None], 0.0)
        z_slope = z_slope + jnp.where(hit, gz[third][:, None], 0.0)
    z_value = z_value.astype(jnp.bfloat16)
    left = jnp.concatenate([a_twelve, a_three], axis=1).astype(jnp.bfloat16)
    right = jnp.concatenate([z_value, z_slope.astype(jnp.bfloat16)], axis=0)
    rhs_acc = rhs_acc + jnp.dot(left, right, preferred_element_type=jnp.float32)
    screen_acc = screen_acc + jnp.dot(
        a_screen.astype(jnp.bfloat16), z_value, preferred_element_type=jnp.float32
    )
    return ((rhs_acc, screen_acc), None)


def shards(brick_ids, voxel_offset, fractions, normals, point_weight, tile_count):
    n_slabs = lax.axis_size("gx")
    n_columns = lax.axis_size("yz")
    devices = n_slabs * n_columns
    tiles_here = brick_ids.shape[0]
    tile_len = voxel_offset.shape[1]
    capacity = max(2, (tiles_here + devices - 1) // devices)
    dest = brick_ids[:, 0]
    order = jnp.arange(tiles_here, dtype=jnp.int32)
    valid = order < tile_count[0]
    earlier = (dest[:, None] == dest[None, :]) & valid[None, :] & (order[None, :] < order[:, None])
    rank = jnp.sum(earlier.astype(jnp.int32), axis=1)
    slots = devices * capacity
    target = jnp.where(valid, dest * capacity + rank, slots)
    packed = jnp.concatenate(
        [
            voxel_offset.astype(jnp.float32)[:, None, :],
            fractions,
            normals,
            point_weight[:, None, :],
        ],
        axis=1,
    )
    outbox = jnp.zeros((slots, 8, tile_len), jnp.float32).at[target].set(packed, mode="drop")
    inbox = lax.all_to_all(outbox, ("gx", "yz"), split_axis=0, concat_axis=0, tiled=True)
    group = 16
    blocks = inbox.reshape(slots // group, group, 8, tile_len)
    plane = (BX + 2) * (BY + 2)
    start = (jnp.zeros((plane, BZ), jnp.float32), jnp.zeros((plane, BZ), jnp.float32))
    (rhs_acc, screen_acc), _ = lax.scan(splat_block, start, blocks)
    field = jnp.stack([rhs_acc, screen_acc]).reshape(2, BX + 2, BY + 2, BZ)
    from_below = passed_along(field[:, BX + 1], "gx", 1)
    from_above = passed_along(field[:, 0], "gx", -1)
    field = field.at[:, 1].add(from_below)
    field = field.at[:, BX].add(from_above)
    inner = field[:, 1 : BX + 1]
    from_left = passed_along(inner[:, :, BY + 1], "yz", 1)
    from_right = passed_along(inner[:, :, 0], "yz", -1)
    inner = inner.at[:, :, 1].add(from_left)
    inner = inner.at[:, :, BY].add(from_right)
    result = inner[:, :, 1 : BY + 1]
    return (result[0], result[1])


def solution(mesh):
    return jax.shard_map(
        shards,
        mesh=mesh,
        in_specs=(
            P(("gx", "yz"), None),
            P(("gx", "yz"), None),
            P(("gx", "yz"), None, None),
            P(("gx", "yz"), None, None),
            P(("gx", "yz"), None),
            P(("gx", "yz")),
        ),
        out_specs=(P("gx", "yz", None), P("gx", "yz", None)),
        check_vma=False,
    )
```

profile of v0, /device:TPU:11, one launch (start us, length us, event | category | flops | bytes accessed | tf_op | source)
XLA Modules:
  0.0 166.0 jit_solution(2598200722877755821)
XLA Ops:
  1.3 0.9 convert_bitcast_fusion
  2.2 1.3 pad_maximum_fusion
  3.5 0.6 copy.17
  4.2 0.2 convert_reduce_fusion
  4.4 1.0 broadcast_in_dim.553
  5.4 13.6 %scatter_fusion = f32[128,8,256]{2,1,0:T(8,128)} fusion(f32[128,8,256]{2,1,0:T(8,128)} %broadcast_in_dim.553, s32[128]{0:T(128)S(1)} %fusion.71, f32[128,8,256]{2,1,0:T(8,128)S(1)} %copy.17), kind=kCustom, calls=%fused_computation | custom fusion | bytes 3146240 | tf_op jit(solution)/shard_map/scatter | solution.py:92
  19.1 6.4 %all-to-all-start = ((f32[128,8,256]{2,1,0:T(8,128)}), f32[128,8,256]{2,1,0:T(8,128)S(1)}, u32[]{:S(2)}, u32[]{:S(2)}) async-start(f32[128,8,256]{2,1,0:T(8,128)} %scatter_fusion), calls=%async_computation | async-start | bytes 2097152 | tf_op jit(solution)/shard_map/all_to_all | solution.py:93
  25.5 25.3 %all-to-all-done = f32[128,8,256]{2,1,0:T(8,128)S(1)} async-done(((f32[128,8,256]{2,1,0:T(8,128)}), f32[128,8,256]{2,1,0:T(8,128)S(1)}, u32[]{:S(2)}, u32[]{:S(2)}) %all-to-all-start) | async-done | bytes 1048608 | tf_op jit(solution)/shard_map/all_to_all | solution.py:93
  50.7 94.3 %while.22 = (s32[]{:T(128)}, f32[60,128]{1,0:T(8,128)S(1)}, f32[60,128]{1,0:T(8,128)S(1)}, f32[8,16,8,256]{3,2,1,0:T(8,128)S(1)}, s32[]{:T(128)}, /*index=5*/s32[]{:T(128)}) while((s32[]{:T(128)}, f32[60,128]{1,0:T(8,128)S(1)}, f32[60,128]{1,0:T(8,128)S(1)}, f32[8,16,8,256]{3,2,1,0:T(8,128)S(1)}, s32[]{:T(128)}, ...), condition=%wide.region_3.4_spmd.clone, body=%wide.region_2.3_spmd.clone.sunk | while | flops 228026368 | bytes 8839260 | solution.py:98
  50.7 0.1 fusion.79
  51.0 3.6 %convolution_add_fusion.2 = f32[60,128]{1,0:T(8,128)S(1)} fusion(f32[4096]{0:T(1024)S(1)} %get-tuple-element.440, f32[4096]{0:T(1024)S(1)} %get-tuple-element.441, f32[4096]{0:T(1024)S(1)} %get-tuple-element.442, f32[4096]{0:T(1024)S(1)} %get-tuple-element.443, f32[4096]{0:T(1024)S(1)} %get-tuple-element.444, f32[4096]{0:T(1024)S(1)} %get-tuple-element.445, ...), kind=kOutput, calls=%fused_computation.11.clone.1 | convolution fusion | flops 74284032 | bytes 454657 | tf_op jit(solution)/shard_map/while/body/eval_jaxpr/dot_general | solution.py:63
  54.6 0.9 add_convert_fusion.16
  55.5 0.9 add_convert_fusion.15
  56.5 5.5 %add_convert_fusion.14 = (bf16[4096,128]{1,0:T(8,128)(2,1)S(1)}, bf16[4096,128]{1,0:T(8,128)(2,1)S(1)}) fusion(f32[4096]{0:T(1024)S(1)} %get-tuple-element.403, s32[4096]{0:T(1024)S(1)} %get-tuple-element.405, f32[4096]{0:T(1024)S(1)} %get-tuple-element.406, s32[4096]{0:T(1024)S(1)} %get-tuple-element.407, f32[4096]{0:T(1024)S(1)} %get-tuple-element.408, ...), kind=kLoop, calls=%fused_computation.6.clone.2 | loop fusion | flops 7864320 | bytes 2244608 | tf_op jit(solution)/shard_map/while/body/eval_jaxpr/convert_element_type | solution.py:59
  62.0 0.5 fusion.80
  62.5 0.1 fusion.79
  62.8 3.6 %convolution_add_fusion.2 = f32[60,128]{1,0:T(8,128)S(1)} fusion(f32[4096]{0:T(1024)S(1)} %get-tuple-element.440, f32[4096]{0:T(1024)S(1)} %get-tuple-element.441, f32[4096]{0:T(1024)S(1)} %get-tuple-element.442, f32[4096]{0:T(1024)S(1)} %get-tuple-element.443, f32[4096]{0:T(1024)S(1)} %get-tuple-element.444, f32[4096]{0:T(1024)S(1)} %get-tuple-element.445, ...), kind=kOutput, calls=%fused_computation.11.clone.1 | convolution fusion | flops 74284032 | bytes 454657 | tf_op jit(solution)/shard_map/while/body/eval_jaxpr/dot_general | solution.py:63
  66.4 0.9 add_convert_fusion.16
  67.3 0.9 add_convert_fusion.15
  68.3 5.5 %add_convert_fusion.14 = (bf16[4096,128]{1,0:T(8,128)(2,1)S(1)}, bf16[4096,128]{1,0:T(8,128)(2,1)S(1)}) fusion(f32[4096]{0:T(1024)S(1)} %get-tuple-element.403, s32[4096]{0:T(1024)S(1)} %get-tuple-element.405, f32[4096]{0:T(1024)S(1)} %get-tuple-element.406, s32[4096]{0:T(1024)S(1)} %get-tuple-element.407, f32[4096]{0:T(1024)S(1)} %get-tuple-element.408, ...), kind=kLoop, calls=%fused_computation.6.clone.2 | loop fusion | flops 7864320 | bytes 2244608 | tf_op jit(solution)/shard_map/while/body/eval_jaxpr/convert_element_type | solution.py:59
  73.8 0.5 fusion.80
  74.3 0.1 fusion.79
  74.6 3.6 %convolution_add_fusion.2 = f32[60,128]{1,0:T(8,128)S(1)} fusion(f32[4096]{0:T(1024)S(1)} %get-tuple-element.440, f32[4096]{0:T(1024)S(1)} %get-tuple-element.441, f32[4096]{0:T(1024)S(1)} %get-tuple-element.442, f32[4096]{0:T(1024)S(1)} %get-tuple-element.443, f32[4096]{0:T(1024)S(1)} %get-tuple-element.444, f32[4096]{0:T(1024)S(1)} %get-tuple-element.445, ...), kind=kOutput, calls=%fused_computation.11.clone.1 | convolution fusion | flops 74284032 | bytes 454657 | tf_op jit(solution)/shard_map/while/body/eval_jaxpr/dot_general | solution.py:63
  78.2 0.9 add_convert_fusion.16
  79.1 0.9 add_convert_fusion.15
  80.0 5.5 %add_convert_fusion.14 = (bf16[4096,128]{1,0:T(8,128)(2,1)S(1)}, bf16[4096,128]{1,0:T(8,128)(2,1)S(1)}) fusion(f32[4096]{0:T(1024)S(1)} %get-tuple-element.403, s32[4096]{0:T(1024)S(1)} %get-tuple-element.405, f32[4096]{0:T(1024)S(1)} %get-tuple-element.406, s32[4096]{0:T(1024)S(1)} %get-tuple-element.407, f32[4096]{0:T(1024)S(1)} %get-tuple-element.408, ...), kind=kLoop, calls=%fused_computation.6.clone.2 | loop fusion | flops 7864320 | bytes 2244608 | tf_op jit(solution)/shard_map/while/body/eval_jaxpr/convert_element_type | solution.py:59
  85.6 0.5 fusion.80
  86.1 0.1 fusion.79
  86.4 3.6 %convolution_add_fusion.2 = f32[60,128]{1,0:T(8,128)S(1)} fusion(f32[4096]{0:T(1024)S(1)} %get-tuple-element.440, f32[4096]{0:T(1024)S(1)} %get-tuple-element.441, f32[4096]{0:T(1024)S(1)} %get-tuple-element.442, f32[4096]{0:T(1024)S(1)} %get-tuple-element.443, f32[4096]{0:T(1024)S(1)} %get-tuple-element.444, f32[4096]{0:T(1024)S(1)} %get-tuple-element.445, ...), kind=kOutput, calls=%fused_computation.11.clone.1 | convolution fusion | flops 74284032 | bytes 454657 | tf_op jit(solution)/shard_map/while/body/eval_jaxpr/dot_general | solution.py:63
  90.0 0.9 add_convert_fusion.16
  90.9 0.9 add_convert_fusion.15
  91.8 5.5 %add_convert_fusion.14 = (bf16[4096,128]{1,0:T(8,128)(2,1)S(1)}, bf16[4096,128]{1,0:T(8,128)(2,1)S(1)}) fusion(f32[4096]{0:T(1024)S(1)} %get-tuple-element.403, s32[4096]{0:T(1024)S(1)} %get-tuple-element.405, f32[4096]{0:T(1024)S(1)} %get-tuple-element.406, s32[4096]{0:T(1024)S(1)} %get-tuple-element.407, f32[4096]{0:T(1024)S(1)} %get-tuple-element.408, ...), kind=kLoop, calls=%fused_computation.6.clone.2 | loop fusion | flops 7864320 | bytes 2244608 | tf_op jit(solution)/shard_map/while/body/eval_jaxpr/convert_element_type | solution.py:59
  97.4 0.5 fusion.80
  97.9 0.1 fusion.79
  98.2 3.6 %convolution_add_fusion.2 = f32[60,128]{1,0:T(8,128)S(1)} fusion(f32[4096]{0:T(1024)S(1)} %get-tuple-element.440, f32[4096]{0:T(1024)S(1)} %get-tuple-element.441, f32[4096]{0:T(1024)S(1)} %get-tuple-element.442, f32[4096]{0:T(1024)S(1)} %get-tuple-element.443, f32[4096]{0:T(1024)S(1)} %get-tuple-element.444, f32[4096]{0:T(1024)S(1)} %get-tuple-element.445, ...), kind=kOutput, calls=%fused_computation.11.clone.1 | convolution fusion | flops 74284032 | bytes 454657 | tf_op jit(solution)/shard_map/while/body/eval_jaxpr/dot_general | solution.py:63
  101.8 0.9 add_convert_fusion.16
  102.7 0.9 add_convert_fusion.15
  103.6 5.5 %add_convert_fusion.14 = (bf16[4096,128]{1,0:T(8,128)(2,1)S(1)}, bf16[4096,128]{1,0:T(8,128)(2,1)S(1)}) fusion(f32[4096]{0:T(1024)S(1)} %get-tuple-element.403, s32[4096]{0:T(1024)S(1)} %get-tuple-element.405, f32[4096]{0:T(1024)S(1)} %get-tuple-element.406, s32[4096]{0:T(1024)S(1)} %get-tuple-element.407, f32[4096]{0:T(1024)S(1)} %get-tuple-element.408, ...), kind=kLoop, calls=%fused_computation.6.clone.2 | loop fusion | flops 7864320 | bytes 2244608 | tf_op jit(solution)/shard_map/while/body/eval_jaxpr/convert_element_type | solution.py:59
  109.2 0.5 fusion.80
  109.7 0.1 fusion.79
  110.0 3.6 %convolution_add_fusion.2 = f32[60,128]{1,0:T(8,128)S(1)} fusion(f32[4096]{0:T(1024)S(1)} %get-tuple-element.440, f32[4096]{0:T(1024)S(1)} %get-tuple-element.441, f32[4096]{0:T(1024)S(1)} %get-tuple-element.442, f32[4096]{0:T(1024)S(1)} %get-tuple-element.443, f32[4096]{0:T(1024)S(1)} %get-tuple-element.444, f32[4096]{0:T(1024)S(1)} %get-tuple-element.445, ...), kind=kOutput, calls=%fused_computation.11.clone.1 | convolution fusion | flops 74284032 | bytes 454657 | tf_op jit(solution)/shard_map/while/body/eval_jaxpr/dot_general | solution.py:63
  113.6 0.9 add_convert_fusion.16
  114.5 0.9 add_convert_fusion.15
  115.4 5.5 %add_convert_fusion.14 = (bf16[4096,128]{1,0:T(8,128)(2,1)S(1)}, bf16[4096,128]{1,0:T(8,128)(2,1)S(1)}) fusion(f32[4096]{0:T(1024)S(1)} %get-tuple-element.403, s32[4096]{0:T(1024)S(1)} %get-tuple-element.405, f32[4096]{0:T(1024)S(1)} %get-tuple-element.406, s32[4096]{0:T(1024)S(1)} %get-tuple-element.407, f32[4096]{0:T(1024)S(1)} %get-tuple-element.408, ...), kind=kLoop, calls=%fused_computation.6.clone.2 | loop fusion | flops 7864320 | bytes 2244608 | tf_op jit(solution)/shard_map/while/body/eval_jaxpr/convert_element_type | solution.py:59
  120.9 0.5 fusion.80
  121.5 0.1 fusion.79
  121.8 3.6 %convolution_add_fusion.2 = f32[60,128]{1,0:T(8,128)S(1)} fusion(f32[4096]{0:T(1024)S(1)} %get-tuple-element.440, f32[4096]{0:T(1024)S(1)} %get-tuple-element.441, f32[4096]{0:T(1024)S(1)} %get-tuple-element.442, f32[4096]{0:T(1024)S(1)} %get-tuple-element.443, f32[4096]{0:T(1024)S(1)} %get-tuple-element.444, f32[4096]{0:T(1024)S(1)} %get-tuple-element.445, ...), kind=kOutput, calls=%fused_computation.11.clone.1 | convolution fusion | flops 74284032 | bytes 454657 | tf_op jit(solution)/shard_map/while/body/eval_jaxpr/dot_general | solution.py:63
  125.4 0.9 add_convert_fusion.16
  126.3 0.9 add_convert_fusion.15
  127.2 5.5 %add_convert_fusion.14 = (bf16[4096,128]{1,0:T(8,128)(2,1)S(1)}, bf16[4096,128]{1,0:T(8,128)(2,1)S(1)}) fusion(f32[4096]{0:T(1024)S(1)} %get-tuple-element.403, s32[4096]{0:T(1024)S(1)} %get-tuple-element.405, f32[4096]{0:T(1024)S(1)} %get-tuple-element.406, s32[4096]{0:T(1024)S(1)} %get-tuple-element.407, f32[4096]{0:T(1024)S(1)} %get-tuple-element.408, ...), kind=kLoop, calls=%fused_computation.6.clone.2 | loop fusion | flops 7864320 | bytes 2244608 | tf_op jit(solution)/shard_map/while/body/eval_jaxpr/convert_element_type | solution.py:59
  132.7 0.5 fusion.80
  133.5 3.6 %convolution_add_fusion.2 = f32[60,128]{1,0:T(8,128)S(1)} fusion(f32[4096]{0:T(1024)S(1)} %get-tuple-element.440, f32[4096]{0:T(1024)S(1)} %get-tuple-element.441, f32[4096]{0:T(1024)S(1)} %get-tuple-element.442, f32[4096]{0:T(1024)S(1)} %get-tuple-element.443, f32[4096]{0:T(1024)S(1)} %get-tuple-element.444, f32[4096]{0:T(1024)S(1)} %get-tuple-element.445, ...), kind=kOutput, calls=%fused_computation.11.clone.1 | convolution fusion | flops 74284032 | bytes 454657 | tf_op jit(solution)/shard_map/while/body/eval_jaxpr/dot_general | solution.py:63
  137.2 0.9 add_convert_fusion.16
  138.1 0.9 add_convert_fusion.15
  139.0 5.5 %add_convert_fusion.14 = (bf16[4096,128]{1,0:T(8,128)(2,1)S(1)}, bf16[4096,128]{1,0:T(8,128)(2,1)S(1)}) fusion(f32[4096]{0:T(1024)S(1)} %get-tuple-element.403, s32[4096]{0:T(1024)S(1)} %get-tuple-element.405, f32[4096]{0:T(1024)S(1)} %get-tuple-element.406, s32[4096]{0:T(1024)S(1)} %get-tuple-element.407, f32[4096]{0:T(1024)S(1)} %get-tuple-element.408, ...), kind=kLoop, calls=%fused_computation.6.clone.2 | loop fusion | flops 7864320 | bytes 2244608 | tf_op jit(solution)/shard_map/while/body/eval_jaxpr/convert_element_type | solution.py:59
  144.5 0.5 fusion.80
  145.1 1.9 %collective-permute-start = (f32[2,10,128]{2,0,1:T(2,128)S(1)}, f32[2,10,128]{2,0,1:T(2,128)S(1)}, u32[]{:S(2)}, u32[]{:S(2)}) collective-permute-start(f32[2,10,128]{2,0,1:T(2,128)S(1)} %fusion.69), channel_id=1, source_target_pairs={{0,8},{8,16},{16,24},{1,9},{9,17},{17,25},{2,10},{10,18},{18,26},{... | collective-permute-start | bytes 30728 | tf_op jit(solution)/shard_map/ppermute | solution.py:14
  147.1 2.4 %collective-permute-done = f32[2,10,128]{2,0,1:T(2,128)S(1)} collective-permute-done((f32[2,10,128]{2,0,1:T(2,128)S(1)}, f32[2,10,128]{2,0,1:T(2,128)S(1)}, u32[]{:S(2)}, u32[]{:S(2)}) %collective-permute-start) | collective-permute-done | bytes 10272 | tf_op jit(solution)/shard_map/ppermute | solution.py:14
  149.6 1.9 %collective-permute-start.1 = (f32[2,10,128]{2,0,1:T(2,128)S(1)}, f32[2,10,128]{2,0,1:T(2,128)S(1)}, u32[]{:S(2)}, u32[]{:S(2)}) collective-permute-start(f32[2,10,128]{2,0,1:T(2,128)S(1)} %get-tuple-element.316), channel_id=1, source_target_pairs={{8,0},{16,8},{24,16},{9,1},{17,9},{25,17},{10,2},{18,10},{26,18},{... | collective-permute-start | bytes 30728 | tf_op jit(solution)/shard_map/ppermute | solution.py:14
  151.5 2.5 %collective-permute-done.1 = f32[2,10,128]{2,0,1:T(2,128)S(1)} collective-permute-done((f32[2,10,128]{2,0,1:T(2,128)S(1)}, f32[2,10,128]{2,0,1:T(2,128)S(1)}, u32[]{:S(2)}, u32[]{:S(2)}) %collective-permute-start.1) | collective-permute-done | bytes 10272 | tf_op jit(solution)/shard_map/ppermute | solution.py:14
  154.1 5.4 %collective-permute-start.2 = (f32[2,4,128]{2,1,0:T(4,128)S(1)}, f32[2,4,128]{2,1,0:T(4,128)S(1)}, u32[]{:S(2)}, u32[]{:S(2)}) collective-permute-start(f32[2,4,128]{2,1,0:T(4,128)S(1)} %get-tuple-element.313), channel_id=1, source_target_pairs={{0,1},{1,2},{2,3},{3,4},{4,5},{5,6},{6,7},{8,9},{9,10},{10,11},{11... | collective-permute-start | bytes 12296 | tf_op jit(solution)/shard_map/ppermute | solution.py:14
  159.5 1.9 %collective-permute-start.3 = (f32[2,4,128]{2,1,0:T(4,128)S(1)}, f32[2,4,128]{2,1,0:T(4,128)S(1)}, u32[]{:S(2)}, u32[]{:S(2)}) collective-permute-start(f32[2,4,128]{2,1,0:T(4,128)S(1)} %get-tuple-element.312), channel_id=1, source_target_pairs={{1,0},{2,1},{3,2},{4,3},{5,4},{6,5},{7,6},{9,8},{10,9},{11,10},{12... | collective-permute-start | bytes 12296 | tf_op jit(solution)/shard_map/ppermute | solution.py:14
  161.5 3.8 %collective-permute-done.3 = f32[2,4,128]{2,1,0:T(4,128)S(1)} collective-permute-done((f32[2,4,128]{2,1,0:T(4,128)S(1)}, f32[2,4,128]{2,1,0:T(4,128)S(1)}, u32[]{:S(2)}, u32[]{:S(2)}) %collective-permute-start.3) | collective-permute-done | bytes 4128 | tf_op jit(solution)/shard_map/ppermute | solution.py:14
  165.4 0.6 slice_bitcast_fusion
  (64 shorter events, 1.7 us)
Async XLA Ops:
  3.5 0.7 copy-start
  19.1 31.7 %all-to-all-start = ((f32[128,8,256]{2,1,0:T(8,128)}), f32[128,8,256]{2,1,0:T(8,128)S(1)}, u32[]{:S(2)}, u32[]{:S(2)}) async-start(f32[128,8,256]{2,1,0:T(8,128)} %scatter_fusion), calls=%async_computation | async-start | bytes 2097152 | tf_op jit(solution)/shard_map/all_to_all | solution.py:93
  145.1 4.4 %collective-permute-start = (f32[2,10,128]{2,0,1:T(2,128)S(1)}, f32[2,10,128]{2,0,1:T(2,128)S(1)}, u32[]{:S(2)}, u32[]{:S(2)}) collective-permute-start(f32[2,10,128]{2,0,1:T(2,128)S(1)} %fusion.69), channel_id=1, source_target_pairs={{0,8},{8,16},{16,24},{1,9},{9,17},{17,25},{2,10},{10,18},{18,26},{... | collective-permute-start | bytes 30728 | tf_op jit(solution)/shard_map/ppermute | solution.py:14
  149.6 4.4 %collective-permute-start.1 = (f32[2,10,128]{2,0,1:T(2,128)S(1)}, f32[2,10,128]{2,0,1:T(2,128)S(1)}, u32[]{:S(2)}, u32[]{:S(2)}) collective-permute-start(f32[2,10,128]{2,0,1:T(2,128)S(1)} %get-tuple-element.316), channel_id=1, source_target_pairs={{8,0},{16,8},{24,16},{9,1},{17,9},{25,17},{10,2},{18,10},{26,18},{... | collective-permute-start | bytes 30728 | tf_op jit(solution)/shard_map/ppermute | solution.py:14
  154.1 7.4 %collective-permute-start.2 = (f32[2,4,128]{2,1,0:T(4,128)S(1)}, f32[2,4,128]{2,1,0:T(4,128)S(1)}, u32[]{:S(2)}, u32[]{:S(2)}) collective-permute-start(f32[2,4,128]{2,1,0:T(4,128)S(1)} %get-tuple-element.313), channel_id=1, source_target_pairs={{0,1},{1,2},{2,3},{3,4},{4,5},{5,6},{6,7},{8,9},{9,10},{10,11},{11... | collective-permute-start | bytes 12296 | tf_op jit(solution)/shard_map/ppermute | solution.py:14
  159.5 5.8 %collective-permute-start.3 = (f32[2,4,128]{2,1,0:T(4,128)S(1)}, f32[2,4,128]{2,1,0:T(4,128)S(1)}, u32[]{:S(2)}, u32[]{:S(2)}) collective-permute-start(f32[2,4,128]{2,1,0:T(4,128)S(1)} %get-tuple-element.312), channel_id=1, source_target_pairs={{1,0},{2,1},{3,2},{4,3},{5,4},{6,5},{7,6},{9,8},{10,9},{11,10},{12... | collective-permute-start | bytes 12296 | tf_op jit(solution)/shard_map/ppermute | solution.py:14
where the time goes:
time: 167 us; the launch traced here: 166 us
  other arithmetic  63 us (38%)
  waiting for transfers between devices  34 us (20%)
  matrix products  33 us (20%)
  starting transfers between devices  17.6 us (11%)
  local copies, waits for them, and re-layouts  16.3 us (10%)
    convert_element_type x8, other arithmetic, splat_block(): z_value = z_value.astype(jnp.bfloat16)  44.1 us
    dot_general x8, matrix products, splat_block(): jnp.dot(a_screen.astype(jnp.bfloat16), z_value, preferred_element_type=jn...  29 us
    all_to_all x1, waiting for transfers between devices, shards(): lax.all_to_all(outbox, ('gx', 'yz'), split_axis=0, concat_axis=0, tiled=T...  25.3 us
    another operation x16, other arithmetic  14.5 us
    scatter x1, local copies, waits for them, and re-layouts, shards(): jnp.zeros((slots, 8, tile_len), jnp.float32).at[target]  13.6 us
    ppermute x4, starting transfers between devices, passed_along(): lax.ppermute(value, axis, [(source, source + steps) for source in range(f...  11.2 us
    ppermute x4, waiting for transfers between devices, passed_along(): lax.ppermute(value, axis, [(source, source + steps) for source in range(f...  8.73 us
    all_to_all x1, starting transfers between devices, shards(): lax.all_to_all(outbox, ('gx', 'yz'), split_axis=0, concat_axis=0, tiled=T...  6.37 us
  transfers between devices with their start and end apart: 5, of which 4 were waited for; matrix products, arithmetic and copies ran while one was open for 0% of the time, Pallas kernels for 0%

commit v1 on v0

v1 whole, which is shorter than its diff:
```python
import functools

import jax
import jax.numpy as jnp
from jax import lax
from jax.experimental import pallas as pl
from jax.experimental.pallas import tpu as pltpu
from jax.sharding import PartitionSpec as P

BX = 4
BY = 8
BZ = 128
MESH = pl.DeviceIdType.MESH
HALO_X = BX + 2
ROWS_Y = 2 * BY
X_CH = 4 * HALO_X
CHANNELS = X_CH + 14


def spline(frac):
    weights = [0.5 * (1.0 - frac) ** 2, 0.75 - (frac - 0.5) ** 2, 0.5 * frac * frac]
    slopes = [frac - 1.0, 1.0 - 2.0 * frac, frac]
    return (weights, slopes)


def pick(masks, values):
    out = jnp.zeros_like(values[0])
    for mask, value in zip(masks, values):
        out = jnp.where(mask, value, out)
    return out


def prepare(rows, off_ref, frac_ref, norm_ref, weight_ref, chan):
    offset = off_ref[rows, :]
    cell_x = offset // (BY * BZ)
    cell_y = (offset // BZ) % BY
    cell_z = offset % BZ
    wx, gx = spline(frac_ref[0, rows, :])
    nx, ny, nz = norm_ref[0, rows, :], norm_ref[1, rows, :], norm_ref[2, rows, :]
    weight = weight_ref[rows, :]
    at = [cell_x == m for m in range(BX)]
    sources = ([nx * v for v in gx], [ny * v for v in wx], [nz * v for v in wx], [weight * v for v in wx])
    for i in range(HALO_X):
        for n, values in enumerate(sources):
            shifts = [k for k in range(3) if 0 <= i - k < BX]
            chan[4 * i + n, rows, :] = pick([at[i - k] for k in shifts], [values[k] for k in shifts])
    wy, gy = spline(frac_ref[1, rows, :])
    wz, gz = spline(frac_ref[2, rows, :])
    rest = [cell_y.astype(jnp.float32)] + wy + gy + [cell_z.astype(jnp.float32)] + wz + gz
    for n, value in enumerate(rest):
        chan[X_CH + n, rows, :] = value


def splat_kernel(
    capacity, n_slabs, n_columns, ids_ref, count_ref, off_ref, frac_ref, norm_ref, weight_ref, out_ref,
    table, used, chan, left, left_n, z_val, z_der, grid
):
    tiles, tile_len = off_ref.shape
    bricks = n_slabs * n_columns
    slots = bricks * capacity

    def clear(q, _):
        table[q] = -1
        return 0

    def clear_used(b, _):
        used[b] = 0
        return 0

    lax.fori_loop(0, slots, clear, 0)
    lax.fori_loop(0, bricks, clear_used, 0)

    def enter(t, _):
        brick = ids_ref[t]
        place = used[brick]
        table[brick * capacity + place] = t
        used[brick] = place + 1
        return 0

    lax.fori_loop(0, count_ref[0], enter, 0)

    def prepare_rows(step, _):
        prepare(pl.ds(pl.multiple_of(step * 8, 8), 8), off_ref, frac_ref, norm_ref, weight_ref, chan)
        return 0

    lax.fori_loop(0, tiles // 8, prepare_rows, 0)
    grid[...] = jnp.zeros_like(grid)

    row_y = lax.broadcasted_iota(jnp.int32, (ROWS_Y, tile_len), 0)
    row_y = jnp.where(row_y == ROWS_Y - 1, -1, row_y).astype(jnp.float32)
    row_z = lax.broadcasted_iota(jnp.int32, (BZ, tile_len), 0).astype(jnp.float32)
    edge = lax.broadcasted_iota(jnp.int32, (HALO_X, BY, BZ), 1)

    def brick_step(b, _):
        for c in range(capacity):
            entry = table[b * capacity + c]
            live = (entry >= 0).astype(jnp.float32)
            tile = jnp.maximum(entry, 0)
            cols = pl.ds(c * tile_len, tile_len)

            def row(n):
                return chan[n, pl.ds(tile, 1), :]

            gap = row_y - row(X_CH)
            hit = [gap == k - 1.0 for k in range(3)]
            wy = pick(hit, [jnp.broadcast_to(row(X_CH + 1 + k) * live, gap.shape) for k in range(3)])
            gy = pick(hit, [jnp.broadcast_to(row(X_CH + 4 + k) * live, gap.shape) for k in range(3)])
            for i in range(HALO_X):
                band = pl.ds(i * ROWS_Y, ROWS_Y)
                low = pl.ds((HALO_X + i) * ROWS_Y, ROWS_Y)
                left[band, cols] = (row(4 * i) * wy + row(4 * i + 1) * gy).astype(jnp.bfloat16)
                left_n[band, cols] = (row(4 * i + 2) * wy).astype(jnp.bfloat16)
                left[low, cols] = (row(4 * i + 3) * wy).astype(jnp.bfloat16)
            gap = row_z - row(X_CH + 7)
            hit = [gap == k - 1.0 for k in range(3)]
            z_val[:, cols] = pick(
                hit, [jnp.broadcast_to(row(X_CH + 8 + k), gap.shape) for k in range(3)]
            ).astype(jnp.bfloat16)
            z_der[:, cols] = pick(
                hit, [jnp.broadcast_to(row(X_CH + 11 + k), gap.shape) for k in range(3)]
            ).astype(jnp.bfloat16)
        dims = (((1,), (1,)), ((), ()))
        both = lax.dot_general(left[...], z_val[...], dims, preferred_element_type=jnp.float32)
        third = lax.dot_general(left_n[...], z_der[...], dims, preferred_element_type=jnp.float32)
        half = HALO_X * ROWS_Y
        fields = (both[:half] + third, both[half:])
        slab, column = b // n_columns, b % n_columns
        above = jnp.where(column == n_columns - 1, n_columns, column + 1)
        below = jnp.where(column == 0, n_columns, column - 1)
        where_x = pl.ds(slab * BX, HALO_X)
        for f, field in enumerate(fields):
            field = field.reshape(HALO_X, ROWS_Y, BZ)
            inner, outer = field[:, :BY], field[:, BY:]
            grid[f, column, where_x] += inner
            grid[f, above, where_x] += jnp.where(edge == 0, outer, 0.0)
            grid[f, below, where_x] += jnp.where(edge == BY - 1, outer, 0.0)
        return 0

    lax.fori_loop(0, bricks, brick_step, 0)
    for f in range(2):
        for column in range(n_columns):
            out_ref[f, column] = grid[f, column, pl.ds(1, n_slabs * BX)]


def splat(capacity, n_slabs, n_columns, ids, count, off, frac, norm, weight):
    tiles, tile_len = off.shape
    bricks = n_slabs * n_columns
    points = capacity * tile_len
    vmem = pl.BlockSpec(memory_space=pltpu.VMEM)
    smem = pl.BlockSpec(memory_space=pltpu.SMEM)
    return pl.pallas_call(
        functools.partial(splat_kernel, capacity, n_slabs, n_columns),
        out_shape=jax.ShapeDtypeStruct((2, n_columns, n_slabs * BX, BY, BZ), jnp.float32),
        in_specs=[smem, smem, vmem, vmem, vmem, vmem],
        out_specs=vmem,
        scratch_shapes=[
            pltpu.SMEM((bricks * capacity,), jnp.int32),
            pltpu.SMEM((bricks,), jnp.int32),
            pltpu.VMEM((CHANNELS, tiles, tile_len), jnp.float32),
            pltpu.VMEM((2 * HALO_X * ROWS_Y, points), jnp.bfloat16),
            pltpu.VMEM((HALO_X * ROWS_Y, points), jnp.bfloat16),
            pltpu.VMEM((BZ, points), jnp.bfloat16),
            pltpu.VMEM((BZ, points), jnp.bfloat16),
            pltpu.VMEM((2, n_columns + 1, n_slabs * BX + 2, BY, BZ), jnp.float32),
        ],
        name="splat",
    )(ids, count, off, frac, norm, weight)


def plan_of(n_slabs, n_columns):
    ybits, xbits = n_columns.bit_length() - 1, n_slabs.bit_length() - 1
    y_rest, x_all = list(range(1, ybits)), [("gx", k) for k in range(xbits)]
    orders = []
    for rest in (y_rest, y_rest[::-1]):
        orders.append([("yz", 0)] * (ybits > 0) + [("yz", k) for k in rest] + x_all)
    axes = [("yz", k) for k in reversed(range(ybits))] + [("gx", k) for k in reversed(range(xbits))]
    return axes, orders


def halving_kernel(n_slabs, n_columns, in_ref, rhs_ref, screen_ref, *scratch):
    axes, orders = plan_of(n_slabs, n_columns)
    steps = len(axes)
    got = (scratch[:steps], scratch[steps : 2 * steps])
    sums = (scratch[2 * steps : 3 * steps], scratch[3 * steps : 4 * steps])
    send_sem, recv_sem = scratch[4 * steps :]
    me = {"gx": lax.axis_index("gx"), "yz": lax.axis_index("yz")}

    def bit_of(axis, k):
        return (me[axis] // (1 << k)) % 2

    def partner(axis, k):
        other = dict(me)
        other[axis] = me[axis] + (1 - 2 * bit_of(axis, k)) * (1 << k)
        return (other["gx"], other["yz"])

    barrier = pltpu.get_barrier_semaphore()
    for axis, k in axes:
        pl.semaphore_signal(barrier, inc=1, device_id=partner(axis, k), device_id_type=MESH)
    pl.semaphore_wait(barrier, steps)

    state = [(in_ref.at[f], list(axes)) for f in range(2)]
    flying = [None, None]

    def begin(f, s):
        ref, left = state[f]
        axis, k = orders[f][s]
        at = left.index((axis, k))
        mine = bit_of(axis, k)
        lead = (slice(None),) * at
        copy = pltpu.make_async_remote_copy(
            src_ref=ref.at[lead + (1 - mine,)],
            dst_ref=got[f][s],
            send_sem=send_sem.at[f, s],
            recv_sem=recv_sem.at[f, s],
            device_id=partner(axis, k),
            device_id_type=MESH,
        )
        copy.start()
        flying[f] = (copy, ref, lead + (mine,), left[:at] + left[at + 1 :])

    for f in range(2):
        begin(f, 0)
    for s in range(steps):
        for f in range(2):
            copy, ref, keep, left = flying[f]
            copy.wait()
            total = ref[keep] + got[f][s][...]
            if s == steps - 1:
                (rhs_ref, screen_ref)[f][...] = total
            else:
                sums[f][s][...] = total
                state[f] = (sums[f][s], left)
                begin(f, s + 1)


def halving(n_slabs, n_columns, field):
    axes, orders = plan_of(n_slabs, n_columns)
    steps = len(axes)
    block = (BX, BY, BZ)
    field = field.reshape((2,) + (2,) * steps + block)
    shapes = [pltpu.VMEM((2,) * (steps - 1 - s) + block, jnp.float32) for s in range(steps)]
    vmem = pl.BlockSpec(memory_space=pltpu.VMEM)
    return pl.pallas_call(
        functools.partial(halving_kernel, n_slabs, n_columns),
        out_shape=[jax.ShapeDtypeStruct(block, jnp.float32)] * 2,
        in_specs=[vmem],
        out_specs=[vmem, vmem],
        scratch_shapes=shapes * 4 + [pltpu.SemaphoreType.DMA((2, steps)), pltpu.SemaphoreType.DMA((2, steps))],
        compiler_params=pltpu.CompilerParams(collective_id=0, has_side_effects=True),
        name="halving",
    )(field)


def shards(brick_ids, voxel_offset, fractions, normals, point_weight, tile_count):
    n_slabs = lax.axis_size("gx")
    n_columns = lax.axis_size("yz")
    devices = n_slabs * n_columns
    tiles_here = brick_ids.shape[0]
    capacity = max(2, (tiles_here + devices - 1) // devices)
    field = splat(
        capacity, n_slabs, n_columns, brick_ids.reshape(tiles_here), tile_count, voxel_offset,
        jnp.transpose(fractions, (1, 0, 2)), jnp.transpose(normals, (1, 0, 2)), point_weight,
    )
    rhs, screen = halving(n_slabs, n_columns, field)
    return (rhs, screen)


def solution(mesh):
    return jax.shard_map(
        shards,
        mesh=mesh,
        in_specs=(
            P(("gx", "yz"), None),
            P(("gx", "yz"), None),
            P(("gx", "yz"), None, None),
            P(("gx", "yz"), None, None),
            P(("gx", "yz"), None),
            P(("gx", "yz")),
        ),
        out_specs=(P("gx", "yz", None), P("gx", "yz", None)),
        check_vma=False,
    )
```

time: 167 us -> 48.3 us (0.29)
  the two profiles are of different devices: /device:TPU:11 before, /device:TPU:0 now
where the time goes in v1:
time: 48.3 us; the launch traced here: 47.9 us
  Pallas kernels  44.7 us (93%)
  local copies, waits for them, and re-layouts  1.94 us (4%)
  between operations  1.3 us (3%)
    pallas_call x1, Pallas kernels, halving(): pl.pallas_call(functools.partial(halving_kernel, n_slabs, n_columns), out...  22.7 us
    pallas_call x1, Pallas kernels, splat(): pl.pallas_call(functools.partial(splat_kernel, capacity, n_slabs, n_colum...  22 us
    unnamed x4, local copies, waits for them, and re-layouts  1.94 us

profile of v1, /device:TPU:0, one launch (start us, length us, event | category | flops | bytes accessed | tf_op | source)
XLA Modules:
  0.0 47.9 jit_solution(2706867988923546282)
XLA Ops:
  1.3 22.0 %splat.1 = f32[2,8,16,8,128]{4,3,2,1,0:T(8,128)} custom-call(s32[128]{0:T(128)} %bitcast.7, s32[1]{0:T(128)S(6)} %copy.10.count_ref, s32[128,256]{1,0:T(8,128)} %off_ref.1, f32[3,128,256]{2,1,0:T(8,128)} %bitcast.5, f32[3,128,256]{2,1,0:T(8,128)} %bitcast.6, f32[128,256]{1,0:T(8,128)} %weight_ref.1), custom_call_target="tpu_custom_call" | custom-call | tf_op jit(solution)/shard_map/splat/pallas_call | solution.py:151
  23.3 22.7 %halving.1 = (f32[4,8,128]{2,1,0:T(8,128)}, f32[4,8,128]{2,1,0:T(8,128)}) custom-call(f32[2,2,2,2,2,2,4,8,128]{8,7,6,5,4,3,2,1,0:T(8,128)} %bitcast.4), custom_call_target="tpu_custom_call" | custom-call | tf_op jit(solution)/shard_map/halving/pallas_call | solution.py:243
  45.9 0.0 copy-start
  46.0 1.3 %copy.11 = f32[4,8,128]{2,1,0:T(8,128)} copy(f32[4,8,128]{2,1,0:T(8,128)} %get-tuple-element.4) | data formatting | bytes 32768
  47.3 0.0 copy-done
  47.3 0.6 %copy.12 = f32[4,8,128]{2,1,0:T(8,128)} copy(f32[4,8,128]{2,1,0:T(8,128)S(1)} %copy-done) | data formatting | bytes 32768
Async XLA Ops:
  45.9 1.3 %copy-start = (f32[4,8,128]{2,1,0:T(8,128)S(1)}, f32[4,8,128]{2,1,0:T(8,128)}, u32[]{:S(2)}) copy-start(f32[4,8,128]{2,1,0:T(8,128)} %get-tuple-element.5) | copy-start | bytes 49156

commit v2 on v1

v2 whole, which is shorter than its diff:
```python
import functools

import jax
import jax.numpy as jnp
from jax import lax
from jax.experimental import pallas as pl
from jax.experimental.pallas import tpu as pltpu
from jax.sharding import PartitionSpec as P

BX = 4
BY = 8
BZ = 128
MESH = pl.DeviceIdType.MESH
HALO_X = BX + 2
ROWS_Y = 2 * BY
X_CH = 4 * HALO_X
CHANNELS = X_CH + 14


def spline(frac):
    weights = [0.5 * (1.0 - frac) ** 2, 0.75 - (frac - 0.5) ** 2, 0.5 * frac * frac]
    slopes = [frac - 1.0, 1.0 - 2.0 * frac, frac]
    return (weights, slopes)


def pick(masks, values):
    out = jnp.zeros_like(values[0])
    for mask, value in zip(masks, values):
        out = jnp.where(mask, value, out)
    return out


def prepare(rows, off_ref, frac_ref, norm_ref, weight_ref, chan):
    offset = off_ref[rows, :]
    cell_x = offset // (BY * BZ)
    cell_y = (offset // BZ) % BY
    cell_z = offset % BZ
    wx, gx = spline(frac_ref[0, rows, :])
    nx, ny, nz = norm_ref[0, rows, :], norm_ref[1, rows, :], norm_ref[2, rows, :]
    weight = weight_ref[rows, :]
    at = [cell_x == m for m in range(BX)]
    sources = ([nx * v for v in gx], [ny * v for v in wx], [nz * v for v in wx], [weight * v for v in wx])
    for i in range(HALO_X):
        for n, values in enumerate(sources):
            shifts = [k for k in range(3) if 0 <= i - k < BX]
            chan[4 * i + n, rows, :] = pick([at[i - k] for k in shifts], [values[k] for k in shifts])
    wy, gy = spline(frac_ref[1, rows, :])
    wz, gz = spline(frac_ref[2, rows, :])
    rest = [cell_y.astype(jnp.float32)] + wy + gy + [cell_z.astype(jnp.float32)] + wz + gz
    for n, value in enumerate(rest):
        chan[X_CH + n, rows, :] = value


def stage_orders(n_columns):
    bits = n_columns.bit_length() - 1
    rest = list(range(1, bits))
    first = [0] if bits else []
    return [first + rest, first + rest[::-1]]


def fused_kernel(
    capacity, n_slabs, n_columns, table_ref, off_ref, frac_ref, norm_ref, weight_ref, rhs_ref, screen_ref,
    chan, left_a, left_b, third_a, third_b, val_a, val_b, der_a, der_b, grid, done, z_main, z_low, z_high,
    send_sem, recv_sem, send_z, recv_z, *stages
):
    tiles, tile_len = off_ref.shape
    orders = stage_orders(n_columns)
    steps = len(orders[0])
    starts = stages[:2]
    got = (stages[2 : 2 + steps], stages[2 + steps : 2 + 2 * steps])
    sums = (stages[2 + 2 * steps : 1 + 3 * steps], stages[1 + 3 * steps : 4 * steps])
    me_x, me_y = lax.axis_index("gx"), lax.axis_index("yz")
    bufs = ((left_a, third_a, val_a, der_a), (left_b, third_b, val_b, der_b))

    def slab_of(step):
        return lax.rem(me_x + 1 + step, n_slabs)

    def bit_of(k):
        return lax.rem(me_y // (1 << k), 2)

    def partner(k):
        return (me_x, me_y + (1 - 2 * bit_of(k)) * (1 << k))

    barrier = pltpu.get_barrier_semaphore()
    for k in range(steps):
        pl.semaphore_signal(barrier, inc=1, device_id=partner(k), device_id_type=MESH)
    for hop in range(1, n_slabs):
        other = (lax.rem(me_x + hop, n_slabs), me_y)
        pl.semaphore_signal(barrier, inc=1, device_id=other, device_id_type=MESH)

    def prepare_rows(step, _):
        prepare(pl.ds(pl.multiple_of(step * 8, 8), 8), off_ref, frac_ref, norm_ref, weight_ref, chan)
        return 0

    lax.fori_loop(0, tiles // 8, prepare_rows, 0)
    grid[...] = jnp.zeros_like(grid)

    row_y = lax.broadcasted_iota(jnp.int32, (ROWS_Y, tile_len), 0)
    row_y = jnp.where(row_y == ROWS_Y - 1, -1, row_y).astype(jnp.float32)
    pack = 16
    row_z = lax.broadcasted_iota(jnp.int32, (pack, tile_len), 0).astype(jnp.float32)
    edge = lax.broadcasted_iota(jnp.int32, (HALO_X, BY, BZ), 1)
    last = n_slabs * n_columns - 1

    def build(g, buf):
        left, third, val, der = buf
        brick = slab_of(g // n_columns) * n_columns + lax.rem(g, n_columns)
        for c in range(capacity):
            entry = table_ref[brick * capacity + c]
            live = (entry >= 0).astype(jnp.float32)
            tile = jnp.maximum(entry, 0)
            cols = pl.ds(c * tile_len, tile_len)

            def row(n):
                return chan[n, pl.ds(tile, 1), :]

            gap = row_y - row(X_CH)
            hit = [gap == k - 1.0 for k in range(3)]
            wy = pick(hit, [jnp.broadcast_to(row(X_CH + 1 + k) * live, gap.shape) for k in range(3)])
            gy = pick(hit, [jnp.broadcast_to(row(X_CH + 4 + k) * live, gap.shape) for k in range(3)])
            for i in range(HALO_X):
                band = pl.ds(i * ROWS_Y, ROWS_Y)
                low = pl.ds((HALO_X + i) * ROWS_Y, ROWS_Y)
                left[band, cols] = (row(4 * i) * wy + row(4 * i + 1) * gy).astype(jnp.bfloat16)
                third[band, cols] = (row(4 * i + 2) * wy).astype(jnp.bfloat16)
                left[low, cols] = (row(4 * i + 3) * wy).astype(jnp.bfloat16)
            wide = [
                jnp.broadcast_to(row(X_CH + 8 + k), row_z.shape).astype(jnp.bfloat16) for k in range(6)
            ]
            base = (row_z - row(X_CH + 7)).astype(jnp.bfloat16)
            for group in range(BZ // pack):
                rows = pl.ds(group * pack, pack)
                hit = [base == jnp.bfloat16(k - 1.0 - group * pack) for k in range(3)]
                val[rows, cols] = pick(hit, wide[:3])
                der[rows, cols] = pick(hit, wide[3:])

    def multiply(g, buf):
        left, third, val, der = buf
        dims = (((1,), (1,)), ((), ()))
        both = lax.dot_general(left[...], val[...], dims, preferred_element_type=jnp.float32)
        part = lax.dot_general(third[...], der[...], dims, preferred_element_type=jnp.float32)
        half = HALO_X * ROWS_Y
        column = lax.rem(g, n_columns)
        above = jnp.where(column == n_columns - 1, n_columns, column + 1)
        below = jnp.where(column == 0, n_columns, column - 1)
        for f, field in enumerate((both[:half] + part, both[half:])):
            field = field.reshape(HALO_X, ROWS_Y, BZ)
            inner, outer = field[:, :BY], field[:, BY:]
            grid[f, column] += inner
            grid[f, above] += jnp.where(edge == 0, outer, 0.0)
            grid[f, below] += jnp.where(edge == BY - 1, outer, 0.0)

    def stage_refs(f, s, j):
        ref = (starts[f] if s == 0 else sums[f][s - 1]).at[j]
        alive = [k for k in reversed(range(steps)) if k not in orders[f][:s]]
        k = orders[f][s]
        lead = (slice(None),) * alive.index(k)
        return ref, lead, k

    def stage_copy(f, s, j):
        ref, lead, k = stage_refs(f, s, j)
        return pltpu.make_async_remote_copy(
            src_ref=ref.at[lead + (1 - bit_of(k),)],
            dst_ref=got[f][s].at[j],
            send_sem=send_sem.at[f, s, j],
            recv_sem=recv_sem.at[f, s, j],
            device_id=partner(k),
            device_id_type=MESH,
        )

    def cross_copy(kind, j):
        source = (done.at[j, :, pl.ds(1, BX)], done.at[j, :, pl.ds(0, 1)], done.at[j, :, pl.ds(BX + 1, 1)])[kind]
        target = (z_main, z_low, z_high)[kind].at[j]
        owner = lax.rem(me_x + (1, n_slabs, 2)[kind] + j, n_slabs)
        return pltpu.make_async_remote_copy(
            src_ref=source,
            dst_ref=target,
            send_sem=send_z.at[kind, j],
            recv_sem=recv_z.at[kind, j],
            device_id=(owner, me_y),
            device_id_type=MESH,
        )

    at_home = (n_slabs - 1, 0, n_slabs - 2)

    def cross_start(kind, j):
        if isinstance(j, int):
            if j != at_home[kind]:
                cross_copy(kind, j).start()
        else:
            @pl.when(j != at_home[kind])
            def _():
                cross_copy(kind, j).start()

    def event(s, j):
        for f in range(2):
            stage_copy(f, s - 1, j).wait()
            ref, lead, k = stage_refs(f, s - 1, j)
            total = ref[lead + (bit_of(k),)] + got[f][s - 1][j]
            if s == steps:
                done[j, f] = total
            else:
                sums[f][s - 1][j] = total
                stage_copy(f, s, j).start()
        if s == steps:
            for kind in range(3):
                cross_start(kind, j)

    build(0, bufs[0])
    pl.semaphore_wait(barrier, steps + n_slabs - 1)
    pairs = n_columns // 4

    def half_step(h, _):
        step, half = h // 2, lax.rem(h, 2)

        def pair(p, _):
            g = (h * pairs + p) * 2
            build(g + 1, bufs[1])
            multiply(g, bufs[0])
            build(jnp.minimum(g + 2, last), bufs[0])
            multiply(g + 1, bufs[1])
            return 0

        lax.fori_loop(0, pairs, pair, 0)

        @pl.when(half == 1)
        def _():
            for f in range(2):
                for column in range(n_columns):
                    bits = tuple((column >> k) & 1 for k in reversed(range(steps)))
                    starts[f][(step,) + bits] = grid[f, column]
                stage_copy(f, 0, step).start()
            grid[...] = jnp.zeros_like(grid)

        for s in range(1, steps + 1):
            @pl.when((half == 0) & (step >= s))
            def _():
                event(s, step - s)

        return 0

    lax.fori_loop(0, 2 * n_slabs, half_step, 0)
    for r in range(1, steps + 1):
        for s in range(r, steps + 1):
            if n_slabs - 1 - (s - r) >= 0:
                event(s, n_slabs - 1 - (s - r))

    main = [done[n_slabs - 1, f, pl.ds(1, BX)] for f in range(2)]
    low = [done[0, f, 0] for f in range(2)]
    high = [done[n_slabs - 2, f, BX + 1] for f in range(2)]
    for j in range(n_slabs):
        for kind in range(3):
            if j != at_home[kind]:
                cross_copy(kind, j).wait()
                for f in range(2):
                    if kind == 0:
                        main[f] = main[f] + z_main[j, f]
                    elif kind == 1:
                        low[f] = low[f] + z_low[j, f, 0]
                    else:
                        high[f] = high[f] + z_high[j, f, 0]
    for f, out in enumerate((rhs_ref, screen_ref)):
        out[...] = main[f]
        out[BX - 1] += jnp.where(me_x < n_slabs - 1, low[f], 0.0)
        out[0] += jnp.where(me_x > 0, high[f], 0.0)


def fused(capacity, n_slabs, n_columns, table, off, frac, norm, weight):
    tiles, tile_len = off.shape
    points = capacity * tile_len
    steps = n_columns.bit_length() - 1
    block = (HALO_X, BY, BZ)
    vmem = pl.BlockSpec(memory_space=pltpu.VMEM)
    smem = pl.BlockSpec(memory_space=pltpu.SMEM)

    def stage(s):
        return pltpu.VMEM((n_slabs,) + (2,) * (steps - s) + block, jnp.float32)

    got = [stage(s + 1) for s in range(steps)]
    sums = [stage(s + 1) for s in range(steps - 1)]
    return pl.pallas_call(
        functools.partial(fused_kernel, capacity, n_slabs, n_columns),
        out_shape=[jax.ShapeDtypeStruct((BX, BY, BZ), jnp.float32)] * 2,
        in_specs=[smem, vmem, vmem, vmem, vmem],
        out_specs=[vmem, vmem],
        scratch_shapes=[pltpu.VMEM((CHANNELS, tiles, tile_len), jnp.float32)]
        + [pltpu.VMEM((2 * HALO_X * ROWS_Y, points), jnp.bfloat16)] * 2
        + [pltpu.VMEM((HALO_X * ROWS_Y, points), jnp.bfloat16)] * 2
        + [pltpu.VMEM((BZ, points), jnp.bfloat16)] * 4
        + [
            pltpu.VMEM((2, n_columns + 1) + block, jnp.float32),
            pltpu.VMEM((n_slabs, 2) + block, jnp.float32),
            pltpu.VMEM((n_slabs, 2, BX, BY, BZ), jnp.float32),
            pltpu.VMEM((n_slabs, 2, 1, BY, BZ), jnp.float32),
            pltpu.VMEM((n_slabs, 2, 1, BY, BZ), jnp.float32),
            pltpu.SemaphoreType.DMA((2, steps, n_slabs)),
            pltpu.SemaphoreType.DMA((2, steps, n_slabs)),
            pltpu.SemaphoreType.DMA((3, n_slabs)),
            pltpu.SemaphoreType.DMA((3, n_slabs)),
        ]
        + [stage(0)] * 2 + got * 2 + sums * 2,
        compiler_params=pltpu.CompilerParams(collective_id=0, has_side_effects=True),
        name="fused",
    )(table, off, frac, norm, weight)


def brick_table(capacity, bricks, dest, count):
    tiles = dest.shape[0]
    order = jnp.arange(tiles, dtype=jnp.int32)
    valid = order < count
    earlier = (dest[:, None] == dest[None, :]) & valid[None, :] & (order[None, :] < order[:, None])
    rank = jnp.sum(earlier.astype(jnp.int32), axis=1)
    slot = jnp.where(valid, dest * capacity + rank, -1)
    slots = jnp.arange(bricks * capacity, dtype=jnp.int32)
    found = jnp.where(slots[:, None] == slot[None, :], order[None, :], -1)
    return jnp.max(found, axis=1)


def shards(brick_ids, voxel_offset, fractions, normals, point_weight, tile_count):
    n_slabs = lax.axis_size("gx")
    n_columns = lax.axis_size("yz")
    devices = n_slabs * n_columns
    tiles_here = brick_ids.shape[0]
    capacity = max(2, (tiles_here + devices - 1) // devices)
    table = brick_table(capacity, devices, brick_ids.reshape(tiles_here), tile_count[0])
    rhs, screen = fused(
        capacity, n_slabs, n_columns, table, voxel_offset,
        jnp.transpose(fractions, (1, 0, 2)), jnp.transpose(normals, (1, 0, 2)), point_weight,
    )
    return (rhs, screen)


def solution(mesh):
    return jax.shard_map(
        shards,
        mesh=mesh,
        in_specs=(
            P(("gx", "yz"), None),
            P(("gx", "yz"), None),
            P(("gx", "yz"), None, None),
            P(("gx", "yz"), None, None),
            P(("gx", "yz"), None),
            P(("gx", "yz")),
        ),
        out_specs=(P("gx", "yz", None), P("gx", "yz", None)),
        check_vma=False,
    )
```

time: 48.3 us -> 36.8 us (0.76)
  Pallas kernels: 44.7 us -> 31.9 us
  other arithmetic: 0 us -> 0.82 us
  local copies, waits for them, and re-layouts: 1.94 us -> 2.57 us
    pallas_call x2 -> x1, Pallas kernels: 44.7 us -> 31.9 us  [fused(): pl.pallas_call(functools.partial(fused_kernel, capacity, n_slabs, n_colum...]
    unnamed x4 -> x6, local copies, waits for them, and re-layouts: 1.94 us -> 2.57 us
    reduce_max x0 -> x1, other arithmetic: none -> 0.63 us  [brick_table(): return jnp.max(found, axis=1)]
where the time goes in v2:
time: 36.8 us; the launch traced here: 36.6 us
  Pallas kernels  31.9 us (87%)
  local copies, waits for them, and re-layouts  2.57 us (7%)
  between operations  1.32 us (4%)
  other arithmetic  0.82 us (2%)
    pallas_call x1, Pallas kernels, fused(): pl.pallas_call(functools.partial(fused_kernel, capacity, n_slabs, n_colum...  31.9 us
    unnamed x6, local copies, waits for them, and re-layouts  2.57 us

profile of v2, /device:TPU:0, one launch (start us, length us, event | category | flops | bytes accessed | tf_op | source)
XLA Modules:
  0.0 36.6 jit_solution(8702019162452182948)
XLA Ops:
  1.3 0.0 copy-start.1
  1.3 0.6 %copy-done.1 = s32[128,1]{0,1:T(1,128)S(1)} copy-done((s32[128,1]{0,1:T(1,128)S(1)}, s32[128,1]{0,1:T(1,128)}, u32[]{:S(2)}) %copy-start.1) | copy-done | bytes 536
  1.9 0.2 convert_reduce_fusion
  2.1 0.6 %select_reduce_fusion.table_ref = s32[128]{0:T(128)} fusion(s32[128]{0:T(128)S(1)} %add_select_fusion), kind=kLoop, calls=%fused_computation | loop fusion | flops 49024 | bytes 1024 | tf_op jit(solution)/shard_map/reduce_max | solution.py:316
  2.8 31.9 %fused.1 = (f32[4,8,128]{2,1,0:T(8,128)}, f32[4,8,128]{2,1,0:T(8,128)}) custom-call(s32[128]{0:T(128)} %select_reduce_fusion.table_ref, s32[128,256]{1,0:T(8,128)} %off_ref.1, f32[3,128,256]{2,1,0:T(8,128)} %bitcast.7, f32[3,128,256]{2,1,0:T(8,128)} %bitcast.8, f32[128,256]{1,0:T(8,128)} %weight_ref.1), custom_call_target="tpu_custom_call" | custom-call | tf_op jit(solution)/shard_map/fused/pallas_call | solution.py:281
  34.7 0.0 copy-start
  34.7 1.3 %copy.11 = f32[4,8,128]{2,1,0:T(8,128)} copy(f32[4,8,128]{2,1,0:T(8,128)} %get-tuple-element.4) | data formatting | bytes 32768
  36.0 0.0 copy-done
  36.0 0.6 %copy.12 = f32[4,8,128]{2,1,0:T(8,128)} copy(f32[4,8,128]{2,1,0:T(8,128)S(1)} %copy-done) | data formatting | bytes 32768
  (2 shorter events, 0.0 us)
Async XLA Ops:
  1.3 0.7 %copy-start.1 = (s32[128,1]{0,1:T(1,128)S(1)}, s32[128,1]{0,1:T(1,128)}, u32[]{:S(2)}) copy-start(s32[128,1]{0,1:T(1,128)} %param.6) | copy-start | bytes 1540
  34.7 1.3 %copy-start = (f32[4,8,128]{2,1,0:T(8,128)S(1)}, f32[4,8,128]{2,1,0:T(8,128)}, u32[]{:S(2)}) copy-start(f32[4,8,128]{2,1,0:T(8,128)} %get-tuple-element.5) | copy-start | bytes 49156

commit v3 on v2

--- a/solution.py
+++ b/solution.py
@@ -14,7 +14,8 @@
 HALO_X = BX + 2
 ROWS_Y = 2 * BY
 X_CH = 4 * HALO_X
-CHANNELS = X_CH + 14
+CHANNELS = X_CH + 19
+PACK = 16
 
 
 def spline(frac):
@@ -31,10 +32,17 @@
 
 
 def prepare(rows, off_ref, frac_ref, norm_ref, weight_ref, chan):
+    parts, lanes = chan.shape[1], chan.shape[3]
+
+    def keep(n, value):
+        for part in range(parts):
+            chan[n, part, rows, :] = value[:, part * lanes : (part + 1) * lanes]
+
     offset = off_ref[rows, :]
-    cell_x = offset // (BY * BZ)
-    cell_y = (offset // BZ) % BY
-    cell_z = offset % BZ
+    z_bits, y_bits = BZ.bit_length() - 1, BY.bit_length() - 1
+    cell_x = offset >> (z_bits + y_bits)
+    cell_y = (offset >> z_bits) & (BY - 1)
+    cell_z = offset & (BZ - 1)
     wx, gx = spline(frac_ref[0, rows, :])
     nx, ny, nz = norm_ref[0, rows, :], norm_ref[1, rows, :], norm_ref[2, rows, :]
     weight = weight_ref[rows, :]
@@ -43,12 +51,15 @@
     for i in range(HALO_X):
         for n, values in enumerate(sources):
             shifts = [k for k in range(3) if 0 <= i - k < BX]
-            chan[4 * i + n, rows, :] = pick([at[i - k] for k in shifts], [values[k] for k in shifts])
+            keep(4 * i + n, pick([at[i - k] for k in shifts], [values[k] for k in shifts]))
     wy, gy = spline(frac_ref[1, rows, :])
     wz, gz = spline(frac_ref[2, rows, :])
-    rest = [cell_y.astype(jnp.float32)] + wy + gy + [cell_z.astype(jnp.float32)] + wz + gz
+    near = [cell_z + (k - 1) for k in range(3)]
+    shift = PACK.bit_length() - 1
+    rest = [cell_y.astype(jnp.float32)] + wy + gy + wz + gz
+    rest += [(z & (PACK - 1)).astype(jnp.float32) for z in near] + [(z >> shift).astype(jnp.float32) for z in near]
     for n, value in enumerate(rest):
-        chan[X_CH + n, rows, :] = value
+        keep(X_CH + n, value)
 
 
 def stage_orders(n_columns):
@@ -95,10 +106,10 @@
     lax.fori_loop(0, tiles // 8, prepare_rows, 0)
     grid[...] = jnp.zeros_like(grid)
 
-    row_y = lax.broadcasted_iota(jnp.int32, (ROWS_Y, tile_len), 0)
+    lanes = tile_len
+    row_y = lax.broadcasted_iota(jnp.int32, (ROWS_Y, lanes), 0)
     row_y = jnp.where(row_y == ROWS_Y - 1, -1, row_y).astype(jnp.float32)
-    pack = 16
-    row_z = lax.broadcasted_iota(jnp.int32, (pack, tile_len), 0).astype(jnp.float32)
+    row_z = lax.broadcasted_iota(jnp.int32, (PACK, lanes), 0).astype(jnp.float32)
     edge = lax.broadcasted_iota(jnp.int32, (HALO_X, BY, BZ), 1)
     last = n_slabs * n_columns - 1
 
@@ -107,32 +118,40 @@
         brick = slab_of(g // n_columns) * n_columns + lax.rem(g, n_columns)
         for c in range(capacity):
             entry = table_ref[brick * capacity + c]
-            live = (entry >= 0).astype(jnp.float32)
+            away = jnp.where(entry >= 0, 0.0, 1.0) * (4.0 * BY)
             tile = jnp.maximum(entry, 0)
-            cols = pl.ds(c * tile_len, tile_len)
-
-            def row(n):
-                return chan[n, pl.ds(tile, 1), :]
-
-            gap = row_y - row(X_CH)
-            hit = [gap == k - 1.0 for k in range(3)]
-            wy = pick(hit, [jnp.broadcast_to(row(X_CH + 1 + k) * live, gap.shape) for k in range(3)])
-            gy = pick(hit, [jnp.broadcast_to(row(X_CH + 4 + k) * live, gap.shape) for k in range(3)])
-            for i in range(HALO_X):
-                band = pl.ds(i * ROWS_Y, ROWS_Y)
-                low = pl.ds((HALO_X + i) * ROWS_Y, ROWS_Y)
-                left[band, cols] = (row(4 * i) * wy + row(4 * i + 1) * gy).astype(jnp.bfloat16)
-                third[band, cols] = (row(4 * i + 2) * wy).astype(jnp.bfloat16)
-                left[low, cols] = (row(4 * i + 3) * wy).astype(jnp.bfloat16)
-            wide = [
-                jnp.broadcast_to(row(X_CH + 8 + k), row_z.shape).astype(jnp.bfloat16) for k in range(6)
-            ]
-            base = (row_z - row(X_CH + 7)).astype(jnp.bfloat16)
-            for group in range(BZ // pack):
-                rows = pl.ds(group * pack, pack)
-                hit = [base == jnp.bfloat16(k - 1.0 - group * pack) for k in range(3)]
-                val[rows, cols] = pick(hit, wide[:3])
-                der[rows, cols] = pick(hit, wide[3:])
+            for part in range(tile_len // lanes):
+                cols = pl.ds(c * tile_len + part * lanes, lanes)
+
+                def row(n):
+                    return chan[n, part, pl.ds(tile, 1), :]
+
+                gap = row_y - (row(X_CH) + away)
+                hit = [gap == k - 1.0 for k in range(3)]
+                wy = pick(hit, [jnp.broadcast_to(row(X_CH + 1 + k), gap.shape) for k in range(3)])
+                gy = pick(hit, [jnp.broadcast_to(row(X_CH + 4 + k), gap.shape) for k in range(3)])
+                for i in range(HALO_X):
+                    band = pl.ds(i * ROWS_Y, ROWS_Y)
+                    low = pl.ds((HALO_X + i) * ROWS_Y, ROWS_Y)
+                    left[band, cols] = (row(4 * i) * wy + row(4 * i + 1) * gy).astype(jnp.bfloat16)
+                    third[band, cols] = (row(4 * i + 2) * wy).astype(jnp.bfloat16)
+                    left[low, cols] = (row(4 * i + 3) * wy).astype(jnp.bfloat16)
+                hit = [row_z == row(X_CH + 13 + k) for k in range(3)]
+
+                def spread(n, other):
+                    for k in range(3):
+                        other = jnp.where(hit[k], jnp.broadcast_to(row(X_CH + n + k), row_z.shape), other)
+                    return other.astype(jnp.bfloat16)
+
+                value = spread(7, jnp.zeros_like(row_z))
+                slope = spread(10, jnp.zeros_like(row_z))
+                home = spread(16, jnp.full_like(row_z, -1.0))
+                zero = jnp.zeros_like(value)
+                for group in range(BZ // PACK):
+                    rows = pl.ds(group * PACK, PACK)
+                    here = home == jnp.bfloat16(group)
+                    val[rows, cols] = jnp.where(here, value, zero)
+                    der[rows, cols] = jnp.where(here, slope, zero)
 
     def multiply(g, buf):
         left, third, val, der = buf
@@ -233,7 +252,7 @@
             grid[...] = jnp.zeros_like(grid)
 
         for s in range(1, steps + 1):
-            @pl.when((half == 0) & (step >= s))
+            @pl.when((half == (0 if s == 1 else 1)) & (step >= s))
             def _():
                 event(s, step - s)
 
@@ -268,6 +287,7 @@
 def fused(capacity, n_slabs, n_columns, table, off, frac, norm, weight):
     tiles, tile_len = off.shape
     points = capacity * tile_len
+    lanes = tile_len
     steps = n_columns.bit_length() - 1
     block = (HALO_X, BY, BZ)
     vmem = pl.BlockSpec(memory_space=pltpu.VMEM)
@@ -283,7 +303,7 @@
         out_shape=[jax.ShapeDtypeStruct((BX, BY, BZ), jnp.float32)] * 2,
         in_specs=[smem, vmem, vmem, vmem, vmem],
         out_specs=[vmem, vmem],
-        scratch_shapes=[pltpu.VMEM((CHANNELS, tiles, tile_len), jnp.float32)]
+        scratch_shapes=[pltpu.VMEM((CHANNELS, tile_len // lanes, tiles, lanes), jnp.float32)]
         + [pltpu.VMEM((2 * HALO_X * ROWS_Y, points), jnp.bfloat16)] * 2
         + [pltpu.VMEM((HALO_X * ROWS_Y, points), jnp.bfloat16)] * 2
         + [pltpu.VMEM((BZ, points), jnp.bfloat16)] * 4

time: 36.8 us -> 35.4 us (0.962)
  Pallas kernels: 31.9 us -> 30.4 us
    pallas_call x1, Pallas kernels: 31.9 us -> 30.4 us  [fused(): pl.pallas_call(functools.partial(fused_kernel, capacity, n_slabs, n_colum...]
where the time goes in v3:
time: 35.4 us; the launch traced here: 35.2 us
  Pallas kernels  30.4 us (86%)
  local copies, waits for them, and re-layouts  2.57 us (7%)
  between operations  1.32 us (4%)
  other arithmetic  0.82 us (2%)
    pallas_call x1, Pallas kernels, fused(): pl.pallas_call(functools.partial(fused_kernel, capacity, n_slabs, n_colum...  30.4 us
    unnamed x6, local copies, waits for them, and re-layouts  2.57 us

profile of v3, /device:TPU:0, one launch (start us, length us, event | category | flops | bytes accessed | tf_op | source)
XLA Modules:
  0.0 35.2 jit_solution(9029594762091974658)
XLA Ops:
  1.3 0.0 copy-start.1
  1.3 0.6 %copy-done.1 = s32[128,1]{0,1:T(1,128)S(1)} copy-done((s32[128,1]{0,1:T(1,128)S(1)}, s32[128,1]{0,1:T(1,128)}, u32[]{:S(2)}) %copy-start.1) | copy-done | bytes 536
  1.9 0.2 convert_reduce_fusion
  2.1 0.6 %select_reduce_fusion.table_ref = s32[128]{0:T(128)} fusion(s32[128]{0:T(128)S(1)} %add_select_fusion), kind=kLoop, calls=%fused_computation | loop fusion | flops 49024 | bytes 1024 | tf_op jit(solution)/shard_map/reduce_max | solution.py:336
  2.8 30.4 %fused.1 = (f32[4,8,128]{2,1,0:T(8,128)}, f32[4,8,128]{2,1,0:T(8,128)}) custom-call(s32[128]{0:T(128)} %select_reduce_fusion.table_ref, s32[128,256]{1,0:T(8,128)} %off_ref.1, f32[3,128,256]{2,1,0:T(8,128)} %bitcast.7, f32[3,128,256]{2,1,0:T(8,128)} %bitcast.8, f32[128,256]{1,0:T(8,128)} %weight_ref.1), custom_call_target="tpu_custom_call" | custom-call | tf_op jit(solution)/shard_map/fused/pallas_call | solution.py:301
  33.2 0.0 copy-start
  33.2 1.3 %copy.11 = f32[4,8,128]{2,1,0:T(8,128)} copy(f32[4,8,128]{2,1,0:T(8,128)} %get-tuple-element.4) | data formatting | bytes 32768
  34.5 0.0 copy-done
  34.5 0.6 %copy.12 = f32[4,8,128]{2,1,0:T(8,128)} copy(f32[4,8,128]{2,1,0:T(8,128)S(1)} %copy-done) | data formatting | bytes 32768
  (2 shorter events, 0.0 us)
Async XLA Ops:
  1.3 0.7 %copy-start.1 = (s32[128,1]{0,1:T(1,128)S(1)}, s32[128,1]{0,1:T(1,128)}, u32[]{:S(2)}) copy-start(s32[128,1]{0,1:T(1,128)} %param.6) | copy-start | bytes 1540
  33.2 1.3 %copy-start = (f32[4,8,128]{2,1,0:T(8,128)S(1)}, f32[4,8,128]{2,1,0:T(8,128)}, u32[]{:S(2)}) copy-start(f32[4,8,128]{2,1,0:T(8,128)} %get-tuple-element.5) | copy-start | bytes 49156

commit v4 on v3

--- a/solution.py
+++ b/solution.py
@@ -70,7 +70,7 @@
 
 
 def fused_kernel(
-    capacity, n_slabs, n_columns, table_ref, off_ref, frac_ref, norm_ref, weight_ref, rhs_ref, screen_ref,
+    capacity, n_slabs, n_columns, table_ref, off_ref, frac_ref, norm_ref, weight_ref, out_ref,
     chan, left_a, left_b, third_a, third_b, val_a, val_b, der_a, der_b, grid, done, z_main, z_low, z_high,
     send_sem, recv_sem, send_z, recv_z, *stages
 ):
@@ -278,7 +278,8 @@
                         low[f] = low[f] + z_low[j, f, 0]
                     else:
                         high[f] = high[f] + z_high[j, f, 0]
-    for f, out in enumerate((rhs_ref, screen_ref)):
+    for f in range(2):
+        out = out_ref.at[f]
         out[...] = main[f]
         out[BX - 1] += jnp.where(me_x < n_slabs - 1, low[f], 0.0)
         out[0] += jnp.where(me_x > 0, high[f], 0.0)
@@ -300,9 +301,9 @@
     sums = [stage(s + 1) for s in range(steps - 1)]
     return pl.pallas_call(
         functools.partial(fused_kernel, capacity, n_slabs, n_columns),
-        out_shape=[jax.ShapeDtypeStruct((BX, BY, BZ), jnp.float32)] * 2,
+        out_shape=jax.ShapeDtypeStruct((2, BX, BY, BZ), jnp.float32),
         in_specs=[smem, vmem, vmem, vmem, vmem],
-        out_specs=[vmem, vmem],
+        out_specs=vmem,
         scratch_shapes=[pltpu.VMEM((CHANNELS, tile_len // lanes, tiles, lanes), jnp.float32)]
         + [pltpu.VMEM((2 * HALO_X * ROWS_Y, points), jnp.bfloat16)] * 2
         + [pltpu.VMEM((HALO_X * ROWS_Y, points), jnp.bfloat16)] * 2
@@ -343,11 +344,11 @@
     tiles_here = brick_ids.shape[0]
     capacity = max(2, (tiles_here + devices - 1) // devices)
     table = brick_table(capacity, devices, brick_ids.reshape(tiles_here), tile_count[0])
-    rhs, screen = fused(
+    both = fused(
         capacity, n_slabs, n_columns, table, voxel_offset,
         jnp.transpose(fractions, (1, 0, 2)), jnp.transpose(normals, (1, 0, 2)), point_weight,
     )
-    return (rhs, screen)
+    return (both[0], both[1])
 
 
 def solution(mesh):

time: 35.4 us -> 34.8 us (0.983)
  local copies, waits for them, and re-layouts: 2.57 us -> 1.99 us
    unnamed x6 -> x2, local copies, waits for them, and re-layouts: 2.57 us -> 0.64 us
    squeeze x0 -> x1, local copies, waits for them, and re-layouts: none -> 1.35 us  [shards(): return (both[0], both[1])]
where the time goes in v4:
time: 34.8 us; the launch traced here: 34.5 us
  Pallas kernels  30.4 us (87%)
  local copies, waits for them, and re-layouts  1.99 us (6%)
  between operations  1.31 us (4%)
  other arithmetic  0.82 us (2%)
    pallas_call x1, Pallas kernels, fused(): pl.pallas_call(functools.partial(fused_kernel, capacity, n_slabs, n_colum...  30.4 us
    squeeze x1, local copies, waits for them, and re-layouts, shards(): return (both[0], both[1])  1.35 us

profile of v4, /device:TPU:0, one launch (start us, length us, event | category | flops | bytes accessed | tf_op | source)
XLA Modules:
  0.0 34.5 jit_solution(13440689004154981174)
XLA Ops:
  1.3 0.0 copy-start
  1.3 0.6 %copy-done = s32[128,1]{0,1:T(1,128)S(1)} copy-done((s32[128,1]{0,1:T(1,128)S(1)}, s32[128,1]{0,1:T(1,128)}, u32[]{:S(2)}) %copy-start) | copy-done | bytes 536
  1.9 0.2 convert_reduce_fusion
  2.1 0.6 %select_reduce_fusion.table_ref = s32[128]{0:T(128)} fusion(s32[128]{0:T(128)S(1)} %add_select_fusion), kind=kLoop, calls=%fused_computation | loop fusion | flops 49024 | bytes 1024 | tf_op jit(solution)/shard_map/reduce_max | solution.py:337
  2.8 30.4 %fused.1 = f32[2,4,8,128]{3,2,1,0:T(8,128)} custom-call(s32[128]{0:T(128)} %select_reduce_fusion.table_ref, s32[128,256]{1,0:T(8,128)} %off_ref.1, f32[3,128,256]{2,1,0:T(8,128)} %bitcast.11, f32[3,128,256]{2,1,0:T(8,128)} %bitcast.12, f32[128,256]{1,0:T(8,128)} %weight_ref.1), custom_call_target="tpu_custom_call" | custom-call | tf_op jit(solution)/shard_map/fused/pallas_call | solution.py:302
  33.2 1.3 %slice_bitcast_fusion = (f32[4,8,128]{2,1,0:T(8,128)}, f32[4,8,128]{2,1,0:T(8,128)}) fusion(f32[2,4,8,128]{3,2,1,0:T(8,128)} %fused.1), kind=kLoop, calls=%fused_computation.5 | loop fusion | bytes 65536 | tf_op jit(solution)/shard_map/squeeze | solution.py:351
  (2 shorter events, 0.0 us)
Async XLA Ops:
  1.3 0.7 %copy-start = (s32[128,1]{0,1:T(1,128)S(1)}, s32[128,1]{0,1:T(1,128)}, u32[]{:S(2)}) copy-start(s32[128,1]{0,1:T(1,128)} %param.6) | copy-start | bytes 1540
